TPU v7x, 32 devices: a 4x4x1 block of a 4x4x8 slice. The times are simulated.
32 devices in a mesh: dp: 1 (over z), tp: 32 (over y, x, core).
Axes of the slice: x: 4, y: 4, z: 1, core: 2. Of those that a mesh axis runs over, the one named last changes fastest.
The devices are a block of a 4x4x8 slice.
Arguments:
- x_in: bfloat16 [2048, 8192], P(('dp', 'tp'))
- w_in: bfloat16 [8192, 28672], P(None, 'tp')
- grad_out: bfloat16 [2048, 28672], P('dp', 'tp')
Outputs:
- output 1: bfloat16 [2048, 8192], P(('dp', 'tp'))
- output 2: float32 [8192, 28672], P('dp', 'tp')
All inputs are finite; a program needn't handle non-finite values.
Results may differ from a plain program's by a relative error of at most 0.001.
Values are sent between devices in bfloat16 or wider.
A program may use at most 768 MiB of HBM per device.

v0:
```python
import jax
import jax.numpy as jnp
from jax import lax
from jax.sharding import PartitionSpec as P


def solution(mesh):
    def per_device(x_blk, w_blk, grad_blk):
        x_full = lax.all_gather(x_blk, "tp", axis=0, tiled=True)
        part_dx = lax.dot_general(grad_blk, w_blk, (((1,), (1,)), ((), ())), preferred_element_type=jnp.float32)
        grad_x = lax.psum_scatter(part_dx, "tp", scatter_dimension=0, tiled=True).astype(jnp.bfloat16)
        grad_w = lax.dot_general(x_full, grad_blk, (((0,), (0,)), ((), ())), preferred_element_type=jnp.float32)
        return grad_x, grad_w

    return jax.shard_map(
        per_device,
        mesh=mesh,
        in_specs=(P(("dp", "tp"), None), P(None, "tp"), P("dp", "tp")),
        out_specs=(P(("dp", "tp"), None), P("dp", "tp")),
        check_vma=False,
    )
```

profile of v0, /device:TPU:97, one launch (start us, length us, event | category | flops | bytes accessed | tf_op | source)
XLA Modules:
  0.0 419.2 jit_solution(9193604068976410902)
XLA Ops:
  7.2 0.1 all-gather.2.cloned.1.call-start
  7.2 0.7 all-gather.2.cloned.1.call-update
  8.0 0.1 reduce-scatter.2.cloned.1.call-start
  8.0 44.6 %fusion = f32[2048,8192]{1,0:T(8,128)} fusion(bf16[2048,896]{1,0:T(8,128)(2,1)} %param.5, bf16[8192,896]{1,0:T(8,128)(2,1)} %param.4), kind=kOutput, calls=%fused_computation | convolution fusion | flops 30064771072 | bytes 85458944 | tf_op jit(solution)/shard_map/dot_general | solution.py:10
  52.6 0.1 reduce-scatter.2.cloned.1.call-update
  52.7 69.9 %all-gather.2.cloned.1.call-done = bf16[2048,8192]{1,0:T(8,128)(2,1)} async-done(((bf16[64,8192]{1,0:T(8,128)(2,1)}), bf16[2048,8192]{1,0:T(8,128)(2,1)}) %all-gather.2.cloned.1.call-update) | async-done | bytes 33554448 | tf_op jit(solution)/shard_map/all_gather | solution.py:9
  122.6 43.4 %fusion.1 = f32[8192,896]{1,0:T(8,128)} fusion(bf16[2048,8192]{1,0:T(8,128)(2,1)} %all-gather.2.cloned.1.call-done, bf16[2048,896]{1,0:T(8,128)(2,1)} %param.5), kind=kOutput, calls=%fused_computation.1 | convolution fusion | flops 30064771072 | bytes 66584576 | tf_op jit(solution)/shard_map/dot_general | solution.py:12
  166.0 243.7 %reduce-scatter.2.cloned.1.call-done = f32[64,8192]{1,0:T(8,128)} async-done(((f32[2048,8192]{1,0:T(8,128)}), f32[64,8192]{1,0:T(8,128)}) %reduce-scatter.2.cloned.1.call-update) | async-done | bytes 2097168 | tf_op jit(solution)/shard_map/reduce_scatter | solution.py:11
  409.7 2.7 convert_element_type.3
Async XLA Ops:
  7.2 115.4 %all-gather.2.cloned.1.call-start = ((), (), s32[]{:S(2)}) async-start(), calls=%async_computation.2 | async-start | bytes 34603008 | tf_op jit(solution)/shard_map/all_gather | solution.py:9
  8.0 401.7 %reduce-scatter.2.cloned.1.call-start = ((), (), s32[]{:S(2)}) async-start(), calls=%async_computation.1 | async-start | bytes 69206016 | tf_op jit(solution)/shard_map/reduce_scatter | solution.py:11
Sparse Core Ops, SparseCore 0:
  10.1 112.4 all-gather.1
  126.5 283.1 reduce-scatter.1
where the time goes:
time: 419 us
  waiting for transfers between devices  314 us (75%)
  matrix products  88 us (21%)
  between operations  14.1 us (3%)
    reduce_scatter x1, waiting for transfers between devices, per_device(): lax.psum_scatter(part_dx, 'tp', scatter_dimension=0, tiled=True)  244 us
    all_gather x1, waiting for transfers between devices, per_device(): x_full = lax.all_gather(x_blk, 'tp', axis=0, tiled=True)  69.9 us
    dot_general x1, matrix products, per_device(): lax.dot_general(grad_blk, w_blk, (((1,), (1,)), ((), ())), preferred_elem...  44.6 us
    dot_general x1, matrix products, per_device(): lax.dot_general(x_full, grad_blk, (((0,), (0,)), ((), ())), preferred_ele...  43.4 us
  transfers between devices with their start and end apart: 2, of which 2 were waited for; matrix products, arithmetic and copies ran while one was open for 21% of the time, Pallas kernels for 0%

commit v1 on v0

v1 whole, which is shorter than its diff:
```python
import functools

import jax
import jax.numpy as jnp
from jax import lax
from jax.experimental import pallas as pl
from jax.experimental.pallas import tpu as pltpu
from jax.sharding import PartitionSpec as P


MESH = pl.DeviceIdType.MESH
OTHER = {"x": "y", "y": "x"}
ORDER = (1, -1, 0)
WAYS = (("x", 1), ("x", -1), ("y", 1), ("y", -1))


def second_axis_kernel(side, *refs):
    own, near, early, late = (refs[4 * i : 4 * i + 4] for i in range(4))
    out_ref, parts, outbox, inbox, mine, theirs, load_sem, send_sem, recv_sem, swap_send, swap_recv, out_sem = refs[16:]
    me = lax.axis_index("tp")
    core, x, y = lax.rem(me, 2), lax.rem(me // 2, side), me // (2 * side)
    chip, width = parts.shape[3], parts.shape[4]
    rows = chip // 2

    def at(yy, xx, cc):
        return ((yy * side) + xx) * 2 + cc

    def neighbour(axis, sign):
        step = 1 if sign > 0 else side - 1
        return at(y, lax.rem(x + step, side), core) if axis == "x" else at(lax.rem(y + step, side), x, core)

    partner = at(y, x, 1 - core)
    barrier = pltpu.get_barrier_semaphore()
    for axis, sign in WAYS:
        pl.semaphore_signal(barrier, inc=1, device_id={"tp": neighbour(axis, sign)}, device_id_type=MESH)
    pl.semaphore_signal(barrier, inc=1, device_id={"tp": partner}, device_id_type=MESH)

    def loads(w, ahead):
        axis, _ = WAYS[w]
        slot = (ahead + side) % side
        b = lax.rem((y if axis == "x" else x) + slot, side)
        last = early[w] if ahead == 2 else late[w].at[ORDER.index(ahead)]
        sources = (own[w].at[b], near[w].at[b], last)
        return [
            pltpu.make_async_copy(src, parts.at[w, slot, i], load_sem.at[w, slot, i]) for i, src in enumerate(sources)
        ]

    for ahead_of in (lambda s: 2, lambda s: -s, lambda s: s, lambda s: 0):
        for w, (axis, sign) in enumerate(WAYS):
            for copy in loads(w, ahead_of(sign)):
                copy.start()

    def arrived(w, ahead):
        for copy in loads(w, ahead):
            copy.wait()
        return parts.at[w, (ahead + side) % side]

    def each(body):
        def step(i, carry):
            body(pl.ds(pl.multiple_of(i * 16, 16), 16))
            return carry

        lax.fori_loop(0, chip // 16, step, 0)

    def send(slot, w, way):
        return pltpu.make_async_remote_copy(
            src_ref=outbox.at[slot, w],
            dst_ref=inbox.at[slot, w],
            send_sem=send_sem.at[slot, w],
            recv_sem=recv_sem.at[slot, w],
            device_id={"tp": neighbour(OTHER[way[0]], way[1])},
            device_id_type=MESH,
        )

    pl.semaphore_wait(barrier, 5)
    for w, way in enumerate(WAYS):
        cell = arrived(w, 2)

        def body(r, cell=cell, w=w):
            outbox[0, w, r, :] = cell[0, r, :] + cell[1, r, :] + cell[2, r, :]

        each(body)
        send(0, w, way).start()
    for w, (axis, sign) in enumerate(WAYS):
        cell = arrived(w ^ 1, sign)

        def body(r, cell=cell, w=w):
            outbox[1, w, r, :] = cell[0, r, :] + cell[1, r, :] + cell[2, r, :]

        each(body)
        send(1, w, (axis, sign)).start()
    for w, way in enumerate(WAYS):
        cell = arrived(w, way[1])
        send(0, w, way).wait_recv()

        def body(r, cell=cell, w=w):
            outbox[2, w, r, :] = cell[0, r, :] + cell[1, r, :] + cell[2, r, :] + inbox[0, w, r, :]

        each(body)
        send(2, w, way).start()

    def swap(w):
        away = pl.ds(pl.multiple_of((1 - core) * rows, rows), rows)
        return pltpu.make_async_remote_copy(
            src_ref=mine.at[w, away],
            dst_ref=theirs.at[w],
            send_sem=swap_send.at[w],
            recv_sem=swap_recv.at[w],
            device_id={"tp": partner},
            device_id_type=MESH,
        )

    def columns(which, w):
        return pl.ds(pl.multiple_of((which * 4 + w) * width, width), width)

    def put(src, which, w, i):
        return pltpu.make_async_copy(src, out_ref.at[:, columns(which, w)], out_sem.at[w, i])

    here = pl.ds(pl.multiple_of(core * rows, rows), rows)
    for w, way in enumerate(WAYS):
        cell = arrived(w, 0)
        send(1, w ^ 1, WAYS[w ^ 1]).wait_recv()
        send(2, w, way).wait_recv()

        def body(r, cell=cell, w=w):
            total = cell[0, r, :] + cell[1, r, :] + cell[2, r, :] + inbox[1, w ^ 1, r, :] + inbox[2, w, r, :]
            mine[w, r, :] = total.astype(mine.dtype)

        each(body)
        swap(w).start()
        put(mine.at[w, here], core, w, 0).start()
    for w, way in enumerate(WAYS):
        swap(w).wait_recv()
        put(theirs.at[w], 1 - core, w, 1).start()
    for w, way in enumerate(WAYS):
        for slot in range(3):
            send(slot, w, way).wait_send()
        swap(w).wait_send()
        put(mine.at[w, here], core, w, 0).wait()
        put(theirs.at[w], 1 - core, w, 1).wait()


def second_axis(side, rows, own, near, early, late):
    _, chip, width = own[0].shape
    sent = 12 * chip * width * 4
    return pl.pallas_call(
        functools.partial(second_axis_kernel, side),
        out_shape=jax.ShapeDtypeStruct((rows, 8 * width), jnp.bfloat16),
        in_specs=[pl.BlockSpec(memory_space=pl.ANY)] * 16,
        out_specs=pl.BlockSpec(memory_space=pl.ANY),
        scratch_shapes=[
            pltpu.VMEM((4, side, 3, chip, width), jnp.float32),
            pltpu.VMEM((3, 4, chip, width), jnp.float32),
            pltpu.VMEM((3, 4, chip, width), jnp.float32),
            pltpu.VMEM((4, chip, width), jnp.bfloat16),
            pltpu.VMEM((4, rows, width), jnp.bfloat16),
            pltpu.SemaphoreType.DMA((4, side, 3)),
            pltpu.SemaphoreType.DMA((3, 4)),
            pltpu.SemaphoreType.DMA((3, 4)),
            pltpu.SemaphoreType.DMA((4,)),
            pltpu.SemaphoreType.DMA((4,)),
            pltpu.SemaphoreType.DMA((4, 2)),
        ],
        compiler_params=pltpu.CompilerParams(
            collective_id=0, has_side_effects=True, vmem_limit_bytes=48 * 1024 * 1024
        ),
        cost_estimate=pl.CostEstimate(flops=20_000_000_000, bytes_accessed=2 * sent, transcendentals=0),
    )(*own, *near, *early, *late)


EVENTS = (0, 8, 16, 22, 34, 44, 58)


def gather_kernel(side, x_ref, w_ref, g_ref, x_full, *refs):
    terms = refs[:16]
    x_own, g_both, w_both, lhs, stage, ring_send, ring_recv, pass_send, pass_recv, swap_send, swap_recv, load_sem, stage_sem = refs[16:]
    me = lax.axis_index("tp")
    core, x, y = lax.rem(me, 2), lax.rem(me // 2, side), me // (2 * side)
    rows, hidden = x_ref.shape
    chip, cols = g_ref.shape[2], g_ref.shape[3]
    half, width, tile = hidden // 2, hidden // 8, stage.shape[3]
    part = 2 * width
    per_term = width // tile

    def at(yy, xx, cc):
        return ((yy * side) + xx) * 2 + cc

    def move(v, step):
        return lax.rem(v + (step + side) % side, side)

    def neighbour(axis, sign):
        return at(y, move(x, sign), core) if axis == "x" else at(move(y, sign), x, core)

    partner = at(y, x, 1 - core)
    barrier = pltpu.get_barrier_semaphore()
    for axis, sign in WAYS:
        pl.semaphore_signal(barrier, inc=1, device_id={"tp": neighbour(axis, sign)}, device_id_type=MESH)
    pl.semaphore_signal(barrier, inc=1, device_id={"tp": partner}, device_id_type=MESH)

    load_x = pltpu.make_async_copy(x_ref, x_own, load_sem.at[0])
    load_g = pltpu.make_async_copy(g_ref, g_both.at[:, :, :, pl.ds(0, cols)], load_sem.at[1])
    load_w = pltpu.make_async_copy(
        w_ref.at[pl.ds(pl.multiple_of(core * half, half), half)], w_both.at[:, pl.ds(0, cols)], load_sem.at[2]
    )
    for copy in (load_x, load_g, load_w):
        copy.start()
    pl.semaphore_wait(barrier, 5)

    def to_partner(src, dst, i):
        return pltpu.make_async_remote_copy(
            src_ref=src, dst_ref=dst, send_sem=swap_send.at[i], recv_sem=swap_recv.at[i],
            device_id={"tp": partner}, device_id_type=MESH,
        )

    load_x.wait()
    my_rows = x_full.at[y, x, pl.ds(pl.multiple_of(core * rows, rows), rows)]
    swap_x = to_partner(x_own, my_rows, 0)
    swap_x.start()
    put_x = pltpu.make_async_copy(x_own, my_rows, load_sem.at[3])
    put_x.start()
    swap_g = to_partner(g_ref, g_both.at[:, :, :, pl.ds(cols, cols)], 1)
    swap_w = to_partner(
        w_ref.at[pl.ds(pl.multiple_of((1 - core) * half, half), half)], w_both.at[:, pl.ds(cols, cols)], 2
    )
    put_x.wait()
    swap_x.wait_recv()

    def cell(p, du, dv, which):
        yy, xx = (move(y, du), move(x, dv)) if p == 0 else (move(y, dv), move(x, du))
        lo = core * half + p * part + (width if which == "B" else 0)
        size = part if which == "all" else width
        return x_full.at[yy, xx, :, pl.ds(pl.multiple_of(lo, width), size)]

    def ring(p, kind, s, du, dv, which):
        first = kind < 2
        axis = ("y" if first else "x") if p == 0 else ("x" if first else "y")
        block = cell(p, du, dv, which)
        return pltpu.make_async_remote_copy(
            src_ref=block, dst_ref=block, send_sem=ring_send.at[p, kind, s], recv_sem=ring_recv.at[p, kind, s],
            device_id={"tp": neighbour(axis, 1 - 2 * s)}, device_id_type=MESH,
        )

    def hand(p, du, dv):
        block, i = cell(p, du, dv, "all"), (du % side) * side + dv % side
        return pltpu.make_async_remote_copy(
            src_ref=block, dst_ref=block, send_sem=pass_send.at[p, i], recv_sem=pass_recv.at[p, i],
            device_id={"tp": partner}, device_id_type=MESH,
        )

    offsets = (0, 1, -1, 2)
    both = [(p, s) for p in range(2) for s in range(2)]

    def u1(p, s):
        return ring(p, 0, s, 0, 0, "all")

    def u2(p, s):
        return ring(p, 1, s, 2 * s - 1, 0, "AB"[s])

    def v1(p, s, k):
        return ring(p, 2 + k, s, offsets[k], 0, "all")

    def v2(p, s, k):
        return ring(p, 6 + k, s, offsets[k], 2 * s - 1, "AB"[s])

    def event0():
        for p, s in both:
            u1(p, s).start()
        for p, s in both:
            v1(p, s, 0).start()
        swap_g.start()
        swap_w.start()
        load_g.wait()
        load_w.wait()
        swap_g.wait_recv()
        swap_w.wait_recv()

    def event1():
        for p, s in both:
            u1(p, s).wait_recv()
        for p, s in both:
            u2(p, s).start()
        for k in (1, 2):
            for p, s in both:
                v1(p, s, k).start()
        for p in range(2):
            hand(p, 1, 0).start()
            hand(p, -1, 0).start()

    def second(k):
        for p, s in both:
            v1(p, s, k).wait_recv()
        for p, s in both:
            v2(p, s, k).start()
        for p in range(2):
            hand(p, offsets[k], 1).start()
            hand(p, offsets[k], -1).start()

    def third(k):
        for p, s in both:
            v2(p, s, k).wait_recv()
        for p in range(2):
            hand(p, offsets[k], 2).start()

    def event2():
        second(0)

    def event3():
        for p, s in both:
            u2(p, s).wait_recv()
        for p, s in both:
            v1(p, s, 3).start()
        for p in range(2):
            hand(p, 2, 0).start()

    def event4():
        second(1)
        third(0)

    def event5():
        second(2)

    def event6():
        second(3)
        third(1)
        third(2)

    events = (event0, event1, event2, event3, event4, event5, event6)

    def stored(slot):
        return pltpu.make_async_copy(stage.at[slot], terms[0].at[:, :, pl.ds(0, tile)], stage_sem.at[slot])

    def step(t, carry):
        for when, event in zip(EVENTS, events):
            pl.when(t == when)(event)
        o, j, slot = t // per_term, lax.rem(t, per_term), lax.rem(t, 2)
        kind, w = o // 4, lax.rem(o, 4)
        ax, sign = w // 2, 1 - 2 * lax.rem(w, 2)
        middle = lax.rem((kind + 1) // 2, 2)
        ahead = 2 * (1 - (kind + 3) // 4) + middle * sign
        q = w + middle * (2 - kind) * sign
        b = lax.rem((1 - ax) * x + ax * y + ahead + side, side)

        @pl.when(j == 0)
        def _():
            for i in range(side):
                lhs[i * chip : (i + 1) * chip, :] = g_both[(1 - ax) * i + ax * b, (1 - ax) * b + ax * i]

        @pl.when(t >= 2)
        def _():
            stored(slot).wait()

        rhs = w_both[pl.ds(pl.multiple_of(q * width + j * tile, tile), tile), :]
        term = lax.dot_general(lhs[...], rhs, (((1,), (1,)), ((), ())), preferred_element_type=jnp.float32)
        stage[slot] = term.reshape(side, chip, tile)
        for i in range(16):

            @pl.when(o == i)
            def _():
                to = terms[i].at[:, :, pl.ds(pl.multiple_of(j * tile, tile), tile)]
                pltpu.make_async_copy(stage.at[slot], to, stage_sem.at[slot]).start()

        return carry

    lax.fori_loop(0, 16 * per_term, step, 0)
    stored(0).wait()
    stored(1).wait()
    third(3)
    for p, s in both:
        u1(p, s).wait_send()
        u2(p, s).wait_send()
        for k in range(4):
            v1(p, s, k).wait_send()
            v2(p, s, k).wait_send()
    for copy in (swap_x, swap_g, swap_w):
        copy.wait_send()
    for p in range(2):
        for du in offsets:
            for dv in offsets:
                if du or dv:
                    hand(p, du, dv).wait()


def gather(side, x_blk, w_blk, g4):
    rows, hidden = x_blk.shape
    chip, cols = g4.shape[2:]
    width = hidden // 8
    tile = 256
    term = jax.ShapeDtypeStruct((side, chip, width), jnp.float32)
    sent = 2 * side * side * chip * hidden
    return pl.pallas_call(
        functools.partial(gather_kernel, side),
        out_shape=[jax.ShapeDtypeStruct((side, side, chip, hidden), x_blk.dtype)] + [term] * 16,
        in_specs=[pl.BlockSpec(memory_space=pl.ANY)] * 3,
        out_specs=[pl.BlockSpec(memory_space=pl.ANY)] * 17,
        scratch_shapes=[
            pltpu.VMEM((rows, hidden), x_blk.dtype),
            pltpu.VMEM((side, side, chip, 2 * cols), g4.dtype),
            pltpu.VMEM((hidden // 2, 2 * cols), w_blk.dtype),
            pltpu.VMEM((side * chip, 2 * cols), g4.dtype),
            pltpu.VMEM((2, side, chip, tile), jnp.float32),
            pltpu.SemaphoreType.DMA((2, 10, 2)),
            pltpu.SemaphoreType.DMA((2, 10, 2)),
            pltpu.SemaphoreType.DMA((2, side * side)),
            pltpu.SemaphoreType.DMA((2, side * side)),
            pltpu.SemaphoreType.DMA((3,)),
            pltpu.SemaphoreType.DMA((3,)),
            pltpu.SemaphoreType.DMA((4,)),
            pltpu.SemaphoreType.DMA((2,)),
        ],
        compiler_params=pltpu.CompilerParams(
            collective_id=1, has_side_effects=True, vmem_limit_bytes=56 * 1024 * 1024
        ),
        cost_estimate=pl.CostEstimate(flops=60_000_000_000, bytes_accessed=2 * sent, transcendentals=0),
    )(x_blk, w_blk, g4)


def solution(mesh):
    n = mesh.shape["tp"]
    side = int(round((n // 2) ** 0.5))

    def device(y, x, core):
        return ((y % side) * side + x % side) * 2 + core

    def shift(axis, step):
        perm = []
        for y in range(side):
            for x in range(side):
                for core in range(2):
                    to = device(y, x + step, core) if axis == "x" else device(y + step, x, core)
                    perm.append((device(y, x, core), to))
        return perm

    def send(t, sign, along):
        return lax.ppermute(t, "tp", shift(along, sign))

    def per_device(x_blk, w_blk, grad_blk):
        me = lax.axis_index("tp")
        pos = {"x": (me // 2) % side, "y": me // (2 * side)}
        rows, hidden = x_blk.shape
        tokens, cols = grad_blk.shape
        chip = tokens // (side * side)

        x_full, *terms = gather(side, x_blk, w_blk, grad_blk.reshape(side, side, chip, cols))
        x_full = x_full.reshape(tokens, hidden)
        terms = {(kind, way): terms[4 * kind + w] for kind in range(4) for w, way in enumerate(WAYS)}

        def cells(t, axis, ahead):
            return lax.dynamic_index_in_dim(t, (pos[OTHER[axis]] + ahead) % side, 0, keepdims=False)

        far, near, early, late = {}, {}, {}, {}
        for axis, sign in WAYS:
            far[axis, sign] = send(terms[0, (axis, sign)], sign, axis)
        for axis, sign in WAYS:
            near[axis, sign] = send(terms[1, (axis, sign)], sign, axis)
        for axis, sign in WAYS:
            t = terms[2, (axis, sign)] + far[axis, sign]
            early[axis, sign] = send(cells(t, axis, 2), sign, axis)
            late[axis, sign] = send(jnp.stack([cells(t, axis, k) for k in ORDER]), sign, axis)

        grad_w = lax.dot_general(x_full, grad_blk, (((0,), (0,)), ((), ())), preferred_element_type=jnp.float32)

        grad_x = second_axis(
            side,
            rows,
            [terms[3, way] for way in WAYS],
            [near[axis, -sign] for axis, sign in WAYS],
            [early[way] for way in WAYS],
            [late[way] for way in WAYS],
        )
        return grad_x, grad_w

    return jax.shard_map(
        per_device,
        mesh=mesh,
        in_specs=(P(("dp", "tp"), None), P(None, "tp"), P("dp", "tp")),
        out_specs=(P(("dp", "tp"), None), P("dp", "tp")),
        check_vma=False,
    )
```

time: 419 us -> 300 us (0.72)
  waiting for transfers between devices: 314 us -> 84.5 us
  Pallas kernels: 0 us -> 146 us
  matrix products: 88 us -> 42.2 us
  starting transfers between devices: 0.12 us -> 15.6 us
  between operations: 14.1 us -> 0.81 us
  other arithmetic: 2.66 us -> 7.68 us
    reduce_scatter x1 -> x0, waiting for transfers between devices: 244 us -> none  [per_device(): lax.psum_scatter(part_dx, 'tp', scatter_dimension=0, tiled=True)]
    pallas_call x0 -> x2, Pallas kernels: none -> 146 us  [the longest x1 102 us: gather(): pl.pallas_call(functools.partial(gather_kernel, side), out_shape=[jax.Sha...]
    ppermute x0 -> x16, waiting for transfers between devices: none -> 84.5 us  [send(): return lax.ppermute(t, 'tp', shift(along, sign))]
    all_gather x1 -> x0, waiting for transfers between devices: 69.9 us -> none  [per_device(): x_full = lax.all_gather(x_blk, 'tp', axis=0, tiled=True)]
    dot_general x1 -> x0, matrix products: 44.6 us -> none  [per_device(): lax.dot_general(grad_blk, w_blk, (((1,), (1,)), ((), ())), preferred_elem...]
    ppermute x0 -> x16, starting transfers between devices: none -> 15.6 us  [send(): return lax.ppermute(t, 'tp', shift(along, sign))]
    add x0 -> x4, other arithmetic: none -> 7.27 us  [per_device(): t = terms[2, (axis, sign)] + far[axis, sign]]
  transfers between devices with their start and end apart: 2 -> 16, of which waited for: 2 -> 6; matrix products, arithmetic and copies ran while one was open for 21% -> 17% of each run, Pallas kernels for 0% -> 0%
where the time goes in v1:
time: 300 us
  Pallas kernels  146 us (49%)
  waiting for transfers between devices  84.5 us (28%)
  matrix products  42.2 us (14%)
  starting transfers between devices  15.6 us (5%)
  other arithmetic  7.68 us (3%)
  local copies, waits for them, and re-layouts  3.3 us (1%)
    pallas_call x1, Pallas kernels, gather(): pl.pallas_call(functools.partial(gather_kernel, side), out_shape=[jax.Sha...  102 us
    ppermute x16, waiting for transfers between devices, send(): return lax.ppermute(t, 'tp', shift(along, sign))  84.5 us
    pallas_call x1, Pallas kernels, second_axis(): pl.pallas_call(functools.partial(second_axis_kernel, side), out_shape=jax...  43.5 us
    dot_general x1, matrix products, per_device(): lax.dot_general(x_full, grad_blk, (((0,), (0,)), ((), ())), preferred_ele...  42.2 us
    ppermute x16, starting transfers between devices, send(): return lax.ppermute(t, 'tp', shift(along, sign))  15.6 us
    add x4, other arithmetic, per_device(): t = terms[2, (axis, sign)] + far[axis, sign]  7.27 us
  transfers between devices with their start and end apart: 16, of which 6 were waited for; matrix products, arithmetic and copies ran while one was open for 17% of the time, Pallas kernels for 0%

profile of v1, /device:TPU:97, one launch (start us, length us, event | category | flops | bytes accessed | tf_op | source)
XLA Modules:
  0.0 300.0 jit_solution(16624664285629299721)
XLA Ops:
  0.6 102.4 %shard_map.50 = (bf16[4,4,128,8192]{3,2,1,0:T(8,128)(2,1)}, f32[4,128,1024]{2,1,0:T(8,128)}, f32[4,128,1024]{2,1,0:T(8,128)}, f32[4,128,1024]{2,1,0:T(8,128)}, f...) custom-call(bf16[64,8192]{1,0:T(8,128)(2,1)} %x_ref.1, ...), custom_call_target="tpu_custom_call" | custom-call | flops 60000002048 | bytes 67108864 | tf_op jit(solution)/shard_map/pallas_call | solution.py:390
  103.0 0.1 collective-permute-start.4
  103.2 2.6 collective-permute-start.6
  105.8 0.0 collective-permute-start.8
  105.8 2.7 collective-permute-start.10
  108.5 0.1 collective-permute-start
  108.6 43.2 %collective-permute-done.4 = f32[4,128,1024]{2,1,0:T(8,128)} collective-permute-done((f32[4,128,1024]{2,1,0:T(8,128)}, f32[4,128,1024]{2,1,0:T(8,128)}, u32[]{:S(2)}, u32[]{:S(2)}) %collective-permute-start.4) | collective-permute-done | bytes 2097184 | tf_op jit(solution)/shard_map/ppermute | solution.py:434
  151.7 0.0 collective-permute-start.1
  151.7 0.0 collective-permute-done.6
  151.7 1.3 collective-permute-start.2
  153.0 0.8 collective-permute-done.8
  153.8 0.0 collective-permute-start.3
  153.8 2.8 add.107
  156.6 0.1 copy-done.2
  156.7 2.1 add.111
  158.8 0.1 copy-done.1
  158.9 2.0 add.112
  160.9 0.3 constant_dynamic-slice_fusion.11
  161.2 0.0 collective-permute-done.10
  161.2 0.1 collective-permute-start.5
  161.3 1.2 copy-done
  162.5 0.4 add.117
  162.9 0.2 constant_dynamic-slice_fusion.8
  163.1 0.2 constant_dynamic-slice_fusion.5
  163.4 0.2 constant_dynamic-slice_fusion.2
  163.6 32.0 %collective-permute-done.refs_4_ = f32[4,128,1024]{2,1,0:T(8,128)} collective-permute-done((f32[4,128,1024]{2,1,0:T(8,128)}, f32[4,128,1024]{2,1,0:T(8,128)}, u32[]{:S(2)}, u32[]{:S(2)}) %collective-permute-start) | collective-permute-done | bytes 2097184 | tf_op jit(solution)/shard_map/ppermute | solution.py:434
  195.6 3.4 %collective-permute-start.7 = (f32[128,1024]{1,0:T(8,128)S(1)}, f32[128,1024]{1,0:T(8,128)S(1)}, u32[]{:S(2)}, u32[]{:S(2)}) collective-permute-start(f32[128,1024]{1,0:T(8,128)S(1)} %get-tuple-element.47), channel_id=1, source_target_pairs={{0,6},{1,7},{2,0},{3,1},{4,2},{5,3},{6,4},{7,5},{8,14},{9,15},{10,... | collective-permute-start | bytes 1572872 | tf_op jit(solution)/shard_map/ppermute | solution.py:434
  199.0 0.4 collective-permute-done.1.refs_5_
  199.4 0.0 collective-permute-start.9
  199.4 0.1 pad_maximum_fusion
  199.5 0.1 pad_maximum_fusion.1
  199.6 0.0 copy-start.3
  199.7 0.1 pad_maximum_fusion.2
  199.8 0.1 pad_maximum_fusion.3
  199.9 0.0 collective-permute-done.2.refs_6_
  199.9 2.8 collective-permute-start.11
  202.7 0.0 collective-permute-done.3.refs_7_
  202.7 0.0 collective-permute-start.12
  202.7 7.9 %collective-permute-done.5.refs_8_ = f32[128,1024]{1,0:T(8,128)S(1)} collective-permute-done((f32[128,1024]{1,0:T(8,128)S(1)}, f32[128,1024]{1,0:T(8,128)S(1)}, u32[]{:S(2)}, u32[]{:S(2)}) %collective-permute-start.5) | collective-permute-done | bytes 524320 | tf_op jit(solution)/shard_map/ppermute | solution.py:434
  210.6 0.0 collective-permute-start.14
  210.6 0.2 collective-permute-done.9.refs_10_
  210.8 2.4 collective-permute-start.15
  213.2 42.2 %fusion = f32[8192,896]{1,0:T(8,128)} fusion(bf16[2048,8192]{1,0:T(8,128)(2,1)} %bitcast.13, bf16[2048,896]{1,0:T(8,128)(2,1)S(1)} %copy-done.3), kind=kOutput, calls=%fused_computation.20 | convolution fusion | flops 30064771072 | bytes 66584576 | tf_op jit(solution)/shard_map/dot_general | solution.py:460
  255.5 0.0 collective-permute-done.11.refs_11_
  255.5 0.0 collective-permute-done.12.refs_12_
  255.5 0.0 collective-permute-done.13.refs_13_
  255.5 43.5 %shard_map.51 = bf16[64,8192]{1,0:T(8,128)(2,1)S(1)} custom-call(f32[4,128,1024]{2,1,0:T(8,128)} %get-tuple-element.19.refs_0_, f32[4,128,1024]{2,1,0:T(8,128)} %get-tuple-element.20.refs_1_, f32[4,128,1024]{2,1,0:T(8,128)} %get-tuple-element.21.refs_2_, f32[4,128,1024]{2,1,0:T(8,128)} %get-tuple-element.22.refs_3_, ...), custom_call_target="tpu_custom_call" | custom-call | flops 20000000000 | bytes 12582912 | tf_op jit(solution)/shard_map/pallas_call | solution.py:146
  299.0 1.0 copy.6
  (8 shorter events, 0.0 us)
Async XLA Ops:
  103.0 48.7 %collective-permute-start.4 = (f32[4,128,1024]{2,1,0:T(8,128)}, f32[4,128,1024]{2,1,0:T(8,128)}, u32[]{:S(2)}, u32[]{:S(2)}) collective-permute-start(f32[4,128,1024]{2,1,0:T(8,128)} %get-tuple-element.28), channel_id=1, source_target_pairs={{0,2},{1,3},{2,4},{3,5},{4,6},{5,7},{6,0},{7,1},{8,10},{9,11},{10,... | collective-permute-start | bytes 6291464 | tf_op jit(solution)/shard_map/ppermute | solution.py:434
  103.2 48.6 %collective-permute-start.6 = (f32[4,128,1024]{2,1,0:T(8,128)}, f32[4,128,1024]{2,1,0:T(8,128)}, u32[]{:S(2)}, u32[]{:S(2)}) collective-permute-start(f32[4,128,1024]{2,1,0:T(8,128)} %get-tuple-element.30), channel_id=1, source_target_pairs={{0,6},{1,7},{2,0},{3,1},{4,2},{5,3},{6,4},{7,5},{8,14},{9,15},{10,... | collective-permute-start | bytes 6291464 | tf_op jit(solution)/shard_map/ppermute | solution.py:434
  105.8 48.0 %collective-permute-start.8 = (f32[4,128,1024]{2,1,0:T(8,128)}, f32[4,128,1024]{2,1,0:T(8,128)}, u32[]{:S(2)}, u32[]{:S(2)}) collective-permute-start(f32[4,128,1024]{2,1,0:T(8,128)} %get-tuple-element.32), channel_id=1, source_target_pairs={{0,8},{1,9},{2,10},{3,11},{4,12},{5,13},{6,14},{7,15},{8,16},{9,17... | collective-permute-start | bytes 6291464 | tf_op jit(solution)/shard_map/ppermute | solution.py:434
  105.8 55.3 %collective-permute-start.10 = (f32[4,128,1024]{2,1,0:T(8,128)}, f32[4,128,1024]{2,1,0:T(8,128)S(1)}, u32[]{:S(2)}, u32[]{:S(2)}) collective-permute-start(f32[4,128,1024]{2,1,0:T(8,128)} %get-tuple-element.34), channel_id=1, source_target_pairs={{0,24},{1,25},{2,26},{3,27},{4,28},{5,29},{6,30},{7,31},{8,0},{9,1... | collective-permute-start | bytes 6291464 | tf_op jit(solution)/shard_map/ppermute | solution.py:434
  108.5 87.1 %collective-permute-start = (f32[4,128,1024]{2,1,0:T(8,128)}, f32[4,128,1024]{2,1,0:T(8,128)}, u32[]{:S(2)}, u32[]{:S(2)}) collective-permute-start(f32[4,128,1024]{2,1,0:T(8,128)} %get-tuple-element.23), channel_id=1, source_target_pairs={{0,6},{1,7},{2,0},{3,1},{4,2},{5,3},{6,4},{7,5},{8,14},{9,15},{10,... | collective-permute-start | bytes 6291464 | tf_op jit(solution)/shard_map/ppermute | solution.py:434
  151.7 47.7 %collective-permute-start.1 = (f32[4,128,1024]{2,1,0:T(8,128)}, f32[4,128,1024]{2,1,0:T(8,128)}, u32[]{:S(2)}, u32[]{:S(2)}) collective-permute-start(f32[4,128,1024]{2,1,0:T(8,128)} %get-tuple-element.24), channel_id=1, source_target_pairs={{0,2},{1,3},{2,4},{3,5},{4,6},{5,7},{6,0},{7,1},{8,10},{9,11},{10,... | collective-permute-start | bytes 6291464 | tf_op jit(solution)/shard_map/ppermute | solution.py:434
  151.7 48.2 %collective-permute-start.2 = (f32[4,128,1024]{2,1,0:T(8,128)}, f32[4,128,1024]{2,1,0:T(8,128)}, u32[]{:S(2)}, u32[]{:S(2)}) collective-permute-start(f32[4,128,1024]{2,1,0:T(8,128)} %get-tuple-element.25), channel_id=1, source_target_pairs={{0,24},{1,25},{2,26},{3,27},{4,28},{5,29},{6,30},{7,31},{8,0},{9,1... | collective-permute-start | bytes 6291464 | tf_op jit(solution)/shard_map/ppermute | solution.py:434
  153.8 48.8 %collective-permute-start.3 = (f32[4,128,1024]{2,1,0:T(8,128)}, f32[4,128,1024]{2,1,0:T(8,128)}, u32[]{:S(2)}, u32[]{:S(2)}) collective-permute-start(f32[4,128,1024]{2,1,0:T(8,128)} %get-tuple-element.26), channel_id=1, source_target_pairs={{0,8},{1,9},{2,10},{3,11},{4,12},{5,13},{6,14},{7,15},{8,16},{9,17... | collective-permute-start | bytes 6291464 | tf_op jit(solution)/shard_map/ppermute | solution.py:434
  153.8 2.9 copy-start.2
  156.7 2.2 copy-start.1
  160.9 1.6 copy-start
  161.2 49.4 %collective-permute-start.5 = (f32[128,1024]{1,0:T(8,128)S(1)}, f32[128,1024]{1,0:T(8,128)S(1)}, u32[]{:S(2)}, u32[]{:S(2)}) collective-permute-start(f32[128,1024]{1,0:T(8,128)S(1)} %get-tuple-element.51), channel_id=1, source_target_pairs={{0,2},{1,3},{2,4},{3,5},{4,6},{5,7},{6,0},{7,1},{8,10},{9,11},{10,... | collective-permute-start | bytes 1572872 | tf_op jit(solution)/shard_map/ppermute | solution.py:434
  195.6 14.9 %collective-permute-start.7 = (f32[128,1024]{1,0:T(8,128)S(1)}, f32[128,1024]{1,0:T(8,128)S(1)}, u32[]{:S(2)}, u32[]{:S(2)}) collective-permute-start(f32[128,1024]{1,0:T(8,128)S(1)} %get-tuple-element.47), channel_id=1, source_target_pairs={{0,6},{1,7},{2,0},{3,1},{4,2},{5,3},{6,4},{7,5},{8,14},{9,15},{10,... | collective-permute-start | bytes 1572872 | tf_op jit(solution)/shard_map/ppermute | solution.py:434
  199.4 11.4 %collective-permute-start.9 = (f32[128,1024]{1,0:T(8,128)S(1)}, f32[128,1024]{1,0:T(8,128)S(1)}, u32[]{:S(2)}, u32[]{:S(2)}) collective-permute-start(f32[128,1024]{1,0:T(8,128)S(1)} %get-tuple-element.43), channel_id=1, source_target_pairs={{0,8},{1,9},{2,10},{3,11},{4,12},{5,13},{6,14},{7,15},{8,16},{9,17... | collective-permute-start | bytes 1572872 | tf_op jit(solution)/shard_map/ppermute | solution.py:434
  199.6 13.6 %copy-start.3 = (bf16[2048,896]{1,0:T(8,128)(2,1)S(1)}, bf16[2048,896]{1,0:T(8,128)(2,1)}, u32[]{:S(2)}) copy-start(bf16[2048,896]{1,0:T(8,128)(2,1)} %param.5) | copy-start | bytes 11010052
  199.9 55.6 %collective-permute-start.11 = (f32[128,1024]{1,0:T(8,128)S(1)}, f32[128,1024]{1,0:T(8,128)S(1)}, u32[]{:S(2)}, u32[]{:S(2)}) collective-permute-start(f32[128,1024]{1,0:T(8,128)S(1)} %get-tuple-element.39), channel_id=1, source_target_pairs={{0,24},{1,25},{2,26},{3,27},{4,28},{5,29},{6,30},{7,31},{8,0},{9,1... | collective-permute-start | bytes 1572872 | tf_op jit(solution)/shard_map/ppermute | solution.py:434
  202.7 52.8 %collective-permute-start.12 = (f32[3,128,1024]{2,1,0:T(8,128)S(1)}, f32[3,128,1024]{2,1,0:T(8,128)S(1)}, u32[]{:S(2)}, u32[]{:S(2)}) collective-permute-start(f32[3,128,1024]{2,1,0:T(8,128)S(1)} %pad_maximum_fusion), channel_id=1, source_target_pairs={{0,2},{1,3},{2,4},{3,5},{4,6},{5,7},{6,0},{7,1},{8,10},{9,11},{10,... | collective-permute-start | bytes 4718600 | tf_op jit(solution)/shard_map/ppermute | solution.py:434
  210.6 44.9 %collective-permute-start.13 = (f32[3,128,1024]{2,1,0:T(8,128)S(1)}, f32[3,128,1024]{2,1,0:T(8,128)}, u32[]{:S(2)}, u32[]{:S(2)}) collective-permute-start(f32[3,128,1024]{2,1,0:T(8,128)S(1)} %pad_maximum_fusion.1), channel_id=1, source_target_pairs={{0,6},{1,7},{2,0},{3,1},{4,2},{5,3},{6,4},{7,5},{8,14},{9,15},{10,... | collective-permute-start | bytes 4718600 | tf_op jit(solution)/shard_map/ppermute | solution.py:434
  210.6 44.9 %collective-permute-start.14 = (f32[3,128,1024]{2,1,0:T(8,128)S(1)}, f32[3,128,1024]{2,1,0:T(8,128)}, u32[]{:S(2)}, u32[]{:S(2)}) collective-permute-start(f32[3,128,1024]{2,1,0:T(8,128)S(1)} %pad_maximum_fusion.2), channel_id=1, source_target_pairs={{0,8},{1,9},{2,10},{3,11},{4,12},{5,13},{6,14},{7,15},{8,16},{9,17... | collective-permute-start | bytes 4718600 | tf_op jit(solution)/shard_map/ppermute | solution.py:434
  210.8 44.7 %collective-permute-start.15 = (f32[3,128,1024]{2,1,0:T(8,128)S(1)}, f32[3,128,1024]{2,1,0:T(8,128)}, u32[]{:S(2)}, u32[]{:S(2)}) collective-permute-start(f32[3,128,1024]{2,1,0:T(8,128)S(1)} %pad_maximum_fusion.3), channel_id=1, source_target_pairs={{0,24},{1,25},{2,26},{3,27},{4,28},{5,29},{6,30},{7,31},{8,0},{9,1... | collective-permute-start | bytes 4718600 | tf_op jit(solution)/shard_map/ppermute | solution.py:434
